TPU v7x, 32 devices: a whole 2x2x4 slice. The times are simulated.
32 devices in a mesh: dp: 8 (over z, x), col: 4 (over y, core).
Axes of the slice: x: 2, y: 2, z: 4, core: 2. Of those that a mesh axis runs over, the one named last changes fastest.
Arguments:
- activations: bfloat16 [2, 7168, 8192], P(None, 'dp', 'col'), may hold values from -40 to 40
- cotangent: bfloat16 [2, 7168, 2048], P(None, 'dp'), may hold values from -40 to 40
- master_weights: float32 [2, 2048, 8192], P(None, 'dp', 'col'), may hold values from -6 to 6
- moment_codes: bfloat16 [2, 2048, 8192], P(None, 'dp', 'col'), may hold values from -1 to 1
- square_codes: bfloat16 [2, 2048, 8192], P(None, 'dp', 'col'), may hold values from 0.049804688 to 1
- moment_scales: float32 [2, 2048, 4], P(None, 'dp'), may hold values from 0.05 to 0.5
- square_scales: float32 [2, 2048, 4], P(None, 'dp'), may hold values from 0.005 to 0.05
Outputs:
- new_weights: float32 [2, 2048, 8192], P(None, 'dp', 'col')
- new_moment_codes: bfloat16 [2, 2048, 8192], P(None, 'dp', 'col')
- new_square_codes: bfloat16 [2, 2048, 8192], P(None, 'dp', 'col')
- new_moment_scales: float32 [2, 2048, 4], P(None, 'dp')
- new_square_scales: float32 [2, 2048, 4], P(None, 'dp')
All inputs are finite; a program needn't handle non-finite values. Where the computation divides by a largest or mean magnitude, that divisor is 1e-20 or more.
Results may differ from a plain program's by a relative error of at most 0.001.
Values sent between devices are 32-bit elements; how exact they have to be, the bound alone decides.
A program may use at most 128 MiB of HBM per device.

v0:
```python
import jax
import jax.numpy as jnp
from jax import lax
from jax.sharding import PartitionSpec as P

D = 8192
KV = 2048
BLOCK = 2048
LAYERS = 2
STEP = 10


beta_one = 0.9
beta_two = 0.999
learn_rate = 0.001
decay_rate = 0.1
adam_eps = 1e-08
scale_eps = 1e-06
norm_eps = 1e-06


def local(
    activations, cotangent, master_weights, moment_codes, square_codes, moment_scales, square_scales
):
    layer_count = activations.shape[0]
    shard_rows = master_weights.shape[1]
    shard_cols = master_weights.shape[2]
    block_count = moment_scales.shape[2]
    pieces = []
    for layer_index in range(layer_count):

        def layer_term(row_start, row_count, layer_index=layer_index):
            cot_rows = cotangent[layer_index]
            return lax.dot_general(
                cot_rows,
                activations[layer_index],
                (((0,), (0,)), ((), ())),
                preferred_element_type=jnp.float32,
            )

        pieces.append(
            lax.psum_scatter(
                layer_term(jnp.int32(0), lax.axis_size("dp") * shard_rows),
                "dp",
                scatter_dimension=0,
                tiled=True,
            )
        )
    gradient = jnp.stack(pieces)
    local_sq = jnp.sum(gradient * gradient)
    total_sq = lax.psum(local_sq, ("dp", "col"))
    rms = jnp.sqrt(total_sq / float(LAYERS * KV * D) + norm_eps)
    clip_factor = jnp.minimum(1.0, 1.0 / rms)
    correct_one = 1.0 - beta_one**STEP
    correct_two = 1.0 - beta_two**STEP
    own_block = lax.axis_index("col") * shard_cols // BLOCK
    selector = (jnp.arange(block_count, dtype=jnp.int32) == own_block).astype(jnp.float32)
    outs_weights, outs_mcode, outs_scode, outs_mscale, outs_sscale = ([], [], [], [], [])
    for layer_index in range(layer_count):
        moment_scale = jnp.sum(moment_scales[layer_index] * selector, axis=1)
        square_scale = jnp.sum(square_scales[layer_index] * selector, axis=1)
        old_moment = moment_codes[layer_index].astype(jnp.float32) * moment_scale[:, None]
        old_square = square_codes[layer_index].astype(jnp.float32) * square_scale[:, None]
        grad_now = clip_factor * gradient[layer_index]
        new_moment = beta_one * old_moment + (1.0 - beta_one) * grad_now
        new_square = beta_two * old_square + (1.0 - beta_two) * grad_now * grad_now
        moment_part = jnp.max(jnp.abs(new_moment), axis=1)[:, None] * selector
        square_part = jnp.max(new_square, axis=1)[:, None] * selector
        moment, square, moment_part, square_part = (
            new_moment,
            new_square,
            moment_part,
            square_part,
        )
        moment_max, square_max = lax.pmax((moment_part, square_part), "col")
        moment_div = jnp.sum(moment_max * selector, axis=1)[:, None]
        square_div = jnp.sum(square_max * selector, axis=1)[:, None]
        moment_out = (moment / (moment_div + scale_eps)).astype(jnp.bfloat16)
        square_out = (square / (square_div + scale_eps)).astype(jnp.bfloat16)
        ratio = moment / correct_one / (jnp.sqrt(square / correct_two) + adam_eps)
        weights = master_weights[layer_index]
        results = (weights - learn_rate * (decay_rate * weights + ratio), moment_out, square_out)
        outs_weights.append(results[0])
        outs_mcode.append(results[1])
        outs_scode.append(results[2])
        outs_mscale.append(moment_max)
        outs_sscale.append(square_max)
    return (
        jnp.stack(outs_weights),
        jnp.stack(outs_mcode),
        jnp.stack(outs_scode),
        jnp.stack(outs_mscale),
        jnp.stack(outs_sscale),
    )


def solution(mesh):
    in_specs = (
        P(None, "dp", "col"),
        P(None, "dp", None),
        P(None, "dp", "col"),
        P(None, "dp", "col"),
        P(None, "dp", "col"),
        P(None, "dp", None),
        P(None, "dp", None),
    )
    out_specs = (
        P(None, "dp", "col"),
        P(None, "dp", "col"),
        P(None, "dp", "col"),
        P(None, "dp", None),
        P(None, "dp", None),
    )
    return jax.shard_map(local, mesh=mesh, in_specs=in_specs, out_specs=out_specs, check_vma=False)
```

profile of v0, /device:TPU:0, one launch (start us, length us, event | category | flops | bytes accessed | tf_op | source)
XLA Modules:
  0.0 667.6 jit_solution(5422857121986061875)
XLA Ops:
  7.2 0.0 reduce-scatter.3.cloned.1.call-start
  7.2 15.0 %fusion.4 = f32[2048,2048]{1,0:T(8,128)} fusion(bf16[2,896,2048]{2,1,0:T(8,128)(2,1)} %param.7, bf16[2,896,2048]{2,1,0:T(8,128)(2,1)} %param.8), kind=kOutput, calls=%fused_computation.6 | convolution fusion | flops 7516192768 | bytes 24117248 | tf_op jit(solution)/shard_map/dot_general | solution.py:34
  22.2 0.0 reduce-scatter.3.cloned.1.call-update
  22.2 0.0 reduce-scatter.5.cloned.1.call-start
  22.2 15.0 %fusion.1 = f32[2048,2048]{1,0:T(8,128)} fusion(bf16[2,896,2048]{2,1,0:T(8,128)(2,1)} %param.7, bf16[2,896,2048]{2,1,0:T(8,128)(2,1)} %param.8), kind=kOutput, calls=%fused_computation.3 | convolution fusion | flops 7516192768 | bytes 24117248 | tf_op jit(solution)/shard_map/dot_general | solution.py:34
  37.2 0.0 reduce-scatter.5.cloned.1.call-update
  37.3 267.3 %reduce-scatter.3.cloned.1.call-done = f32[256,2048]{1,0:T(8,128)} async-done(((f32[2048,2048]{1,0:T(8,128)}), f32[256,2048]{1,0:T(8,128)}) %reduce-scatter.3.cloned.1.call-update) | async-done | bytes 2097168 | tf_op jit(solution)/shard_map/reduce_scatter | solution.py:42
  304.5 282.6 %reduce-scatter.5.cloned.1.call-done = f32[256,2048]{1,0:T(8,128)} async-done(((f32[2048,2048]{1,0:T(8,128)}), f32[256,2048]{1,0:T(8,128)}) %reduce-scatter.5.cloned.1.call-update) | async-done | bytes 2097168 | tf_op jit(solution)/shard_map/reduce_scatter | solution.py:42
  587.2 0.0 copy-start.1
  587.2 0.0 copy-start.2
  587.2 0.0 copy-start
  587.2 4.1 fusion
  591.2 0.0 copy-done.1
  591.2 0.0 copy-done.2
  591.2 0.1 fusion.31
  591.3 39.7 %psum.7 = f32[]{:T(128)} all-reduce(f32[]{:T(128)} %fusion), channel_id=1, replica_groups=mesh['dp'=8,'col'=4] {'dp','col'}, use_global_device_ids=true, to_apply=%region_4.5 | all-reduce | flops 1 | bytes 8 | tf_op jit(solution)/shard_map/psum | solution.py:51
  631.7 0.0 copy-done
  631.8 8.3 %fusion.24 = (f32[1,256,2048]{2,1,0:T(8,128)S(1)}, f32[1,256,2048]{2,1,0:T(8,128)S(1)}, f32[256]{0:T(256)S(1)}, f32[256]{0:T(256)S(1)}, f32[256]{0:T(256)S(1)}, /*index=5*/f32[256]{0:T(256)S(1)}) fusion(f32[2,256,2048]{2,1,0:T(8,128)} %param.9, f32[256,2048]{1,0:T(8,128)S(1)} %copy-done, f32[]{:T(128)S(6)} %min.3, f32[256]{0:T(256)S(1)} %get-tuple-element.18, ...), kind=kLoop, calls=%fused_computation.38 | loop fusion | flops 24116224 | bytes 16785412 | tf_op jit(solution)/shard_map/stack | solution.py:89
  640.0 2.5 pad_maximum_fusion
  642.5 0.1 broadcast_multiply_fusion
  642.6 10.3 %all-reduce = (f32[256,4]{0,1:T(4,128)S(1)}, f32[256,4]{0,1:T(4,128)S(1)}, f32[256,4]{0,1:T(4,128)S(1)}, f32[256,4]{0,1:T(4,128)S(1)}) all-reduce(f32[256,4]{0,1:T(4,128)S(1)} %get-tuple-element.35, f32[256,4]{0,1:T(4,128)S(1)} %get-tuple-element.34, f32[256,4]{0,1:T(4,128)S(1)} %get-tuple-element.36, ...), channel_id=1, replica_groups=mesh['dp'=8,'col'=4] {'col'}, use_global_device_ids=true, to_apply=%region_15.16 | all-reduce | flops 4096 | bytes 32768 | tf_op jit(solution)/shard_map/pmax | solution.py:75
  653.0 0.1 multiply_reduce_fusion.1
  653.1 4.1 fusion.27
  657.1 1.5 pad_maximum_fusion.1
  658.6 1.5 pad_maximum_fusion.2
  660.1 0.6 pad_maximum_fusion.3
  (3 shorter events, 0.0 us)
Async XLA Ops:
  7.2 297.3 %reduce-scatter.3.cloned.1.call-start = ((), (), s32[]{:S(2)}) async-start(), calls=%async_computation.2 | async-start | bytes 18874368 | tf_op jit(solution)/shard_map/reduce_scatter | solution.py:42
  22.2 565.0 %reduce-scatter.5.cloned.1.call-start = ((), (), s32[]{:S(2)}) async-start(), calls=%async_computation.3 | async-start | bytes 18874368 | tf_op jit(solution)/shard_map/reduce_scatter | solution.py:42
  587.2 4.1 copy-start.1
  587.2 4.1 copy-start.2
  587.2 44.6 %copy-start = (f32[256,2048]{1,0:T(8,128)S(1)}, f32[256,2048]{1,0:T(8,128)}, u32[]{:S(2)}) copy-start(f32[256,2048]{1,0:T(8,128)} %reduce-scatter.3.cloned.1.call-done) | copy-start | bytes 6291460
Sparse Core Ops, SparseCore 0:
  22.3 282.1 reduce-scatter.2
  308.3 278.8 reduce-scatter.4
where the time goes:
time: 668 us
  waiting for transfers between devices  550 us (82%)
  blocking collectives  50.1 us (8%)
  matrix products  29.9 us (4%)
  other arithmetic  22.8 us (3%)
  between operations  14.8 us (2%)
    reduce_scatter x2, waiting for transfers between devices, local(): lax.psum_scatter(layer_term(jnp.int32(0), lax.axis_size('dp') * shard_row...  550 us
    psum x1, blocking collectives, local(): total_sq = lax.psum(local_sq, ('dp', 'col'))  39.7 us
    dot_general x2, matrix products, layer_term(): lax.dot_general(cot_rows, activations[layer_index], (((0,), (0,)), ((), (...  29.9 us
  transfers between devices with their start and end apart: 2, of which 2 were waited for; matrix products, arithmetic and copies ran while one was open for 2% of the time, Pallas kernels for 0%

commit v1 on v0

--- a/solution.py
+++ b/solution.py
@@ -1,6 +1,10 @@
+import functools
+
 import jax
 import jax.numpy as jnp
 from jax import lax
+from jax.experimental import pallas as pl
+from jax.experimental.pallas import tpu as pltpu
 from jax.sharding import PartitionSpec as P
 
 D = 8192
@@ -18,37 +22,334 @@
 scale_eps = 1e-06
 norm_eps = 1e-06
 
+LANES = 128
+AHEAD = 3
+XSLOTS = 4
+
+
+def reduce_kernel(
+    count, col_count, cot_ref, act_ref, out_ref, sq_ref,
+    xs, xr, part, arr, bs, br, own_sq, sum_sq, col_sq, dp_sq,
+    xs_sem, xr_sem, rs_sem, rr_sem, ls_sem, ll_sem, bs_sem, br_sem,
+    cs_sem, cr_sem, ds_sem, dr_sem, x_free, from_right, from_left,
+):
+    layers, pairs, line, rows, tokens = cot_ref.shape
+    cols = act_ref.shape[2]
+    slots = part.shape[0]
+    wide_per = cols // (2 * LANES) - 1
+    per_layer = wide_per + 2
+    period = (per_layer + 1) // 2
+    items = layers * per_layer
+    wides = layers * wide_per
+    me = lax.axis_index("dp")
+    z = me // 2
+    x = me % 2
+    peer = 2 * z + 1 - x
+    right = jnp.minimum(z + 1, line - 1) * 2 + x
+    left = jnp.maximum(z - 1, 0) * 2 + x
+    has_right = z < line - 1
+    has_left = z > 0
+    mirror = line - 1 - z
+
+    def signal(sem, where):
+        pl.semaphore_signal(
+            sem, inc=1, device_id={"dp": where}, device_id_type=pl.DeviceIdType.MESH
+        )
+
+    barrier = pltpu.get_barrier_semaphore()
+    mine = lax.axis_index("col")
+    for offset in range(1, count):
+        signal(barrier, lax.rem(me + offset, count))
+    for offset in range(1, col_count):
+        pl.semaphore_signal(
+            barrier, inc=1, device_id={"col": lax.rem(mine + offset, col_count)},
+            device_id_type=pl.DeviceIdType.MESH,
+        )
+    pl.semaphore_wait(barrier, count + col_count - 2)
+
+    def remote(src, dst, send, recv, where):
+        return pltpu.make_async_remote_copy(
+            src_ref=src, dst_ref=dst, send_sem=send, recv_sem=recv,
+            device_id={"dp": where}, device_id_type=pl.DeviceIdType.MESH,
+        )
+
+    def describe(item):
+        layer = item // per_layer
+        place = item % per_layer
+        narrow = place % period == 0
+        wide_at = place - (place + period - 1) // period
+        narrow_at = place // period
+        return layer, narrow, wide_at, narrow_at
+
+    def x_copy(number):
+        slot = number % XSLOTS
+        return remote(xs.at[slot], xr.at[slot], xs_sem.at[slot], xr_sem.at[slot], peer)
+
+    def r_copy(slot, target):
+        return remote(
+            part.at[slot, target], arr.at[slot, target + 1],
+            rs_sem.at[slot, target], rr_sem.at[slot, target], right,
+        )
+
+    def l_copy(slot, target):
+        return remote(
+            part.at[slot, target], arr.at[slot, target],
+            ls_sem.at[slot, target], ll_sem.at[slot, target], left,
+        )
+
+    def b_copy(number):
+        return remote(
+            bs.at[number], br.at[number], bs_sem.at[number], br_sem.at[number], peer
+        )
+
+    def product(layer, pair, target, start, width):
+        return jnp.dot(
+            cot_ref[layer, pair, target],
+            act_ref[layer, :, pl.ds(pl.multiple_of(start, LANES), width)],
+            preferred_element_type=jnp.float32,
+        )
+
+    def send_wide(item):
+        layer, narrow, wide_at, _ = describe(item)
+
+        @pl.when(jnp.logical_not(narrow))
+        def _():
+            number = layer * wide_per + wide_at
+            slot = number % XSLOTS
+
+            @pl.loop(0, line)
+            def _(target):
+                value = product(layer, 1 - x, target, wide_at * 2 * LANES, 2 * LANES)
+                xs[slot, target, 0] = value[:, :LANES]
+                xs[slot, target, 1] = value[:, LANES:]
+
+            @pl.when(number >= XSLOTS)
+            def _():
+                pl.semaphore_wait(x_free, 1)
+
+            x_copy(number).start()
+
+    def form(item):
+        layer, narrow, wide_at, narrow_at = describe(item)
+        here = item % slots
+
+        @pl.when(item >= slots)
+        def _():
+            @pl.when(has_right)
+            def _():
+                pl.semaphore_wait(from_right, 1)
+
+            @pl.when(has_left)
+            def _():
+                pl.semaphore_wait(from_left, 1)
+
+        @pl.when(narrow)
+        def _():
+            start = wide_per * 2 * LANES + narrow_at * LANES
+
+            @pl.loop(0, line)
+            def _(target):
+                part[here, target, 0] = product(layer, 0, target, start, LANES)
+                part[here, target, 1] = product(layer, 1, target, start, LANES)
+
+        @pl.when(jnp.logical_not(narrow))
+        def _():
+            number = layer * wide_per + wide_at
+            slot = number % XSLOTS
+            x_copy(number).wait()
+
+            @pl.loop(0, line)
+            def _(target):
+                value = product(layer, x, target, wide_at * 2 * LANES, 2 * LANES)
+                part[here, target, 0] = value[:, :LANES] + xr[slot, target, 0]
+                part[here, target, 1] = value[:, LANES:] + xr[slot, target, 1]
+
+            @pl.when(number + XSLOTS < wides)
+            def _():
+                signal(x_free, peer)
+
+    def hop(item, stage):
+        here = item % slots
+
+        @pl.when(z <= stage)
+        def _():
+            target = line - 1 - stage + z
+            if stage > 0:
+                @pl.when(has_left)
+                def _():
+                    r_copy(here, target).wait_recv()
+                    part[here, target] += arr[here, target + 1]
+
+            r_copy(here, target).start()
+
+        @pl.when(mirror <= stage)
+        def _():
+            target = stage - mirror
+            if stage > 0:
+                @pl.when(has_right)
+                def _():
+                    l_copy(here, target).wait_recv()
+                    part[here, target] += arr[here, target]
+
+            l_copy(here, target).start()
+
+    def finish(item):
+        layer, narrow, wide_at, narrow_at = describe(item)
+        here = item % slots
+
+        @pl.when(has_left)
+        def _():
+            r_copy(here, z).wait_recv()
+            part[here, z] += arr[here, z + 1]
+
+        @pl.when(has_right)
+        def _():
+            l_copy(here, z).wait_recv()
+            part[here, z] += arr[here, z]
+
+        for target in range(line):
+            @pl.when(target > z)
+            def _(target=target):
+                r_copy(here, target).wait_send()
+
+            @pl.when(target < z)
+            def _(target=target):
+                l_copy(here, target).wait_send()
+
+        @pl.when(narrow)
+        def _():
+            number = layer * 2 + narrow_at
+            start = wide_per * 2 * LANES + narrow_at * LANES
+            bs[number] = part[here, z, 1 - x]
+            b_copy(number).start()
+            out_ref[layer, :, pl.ds(pl.multiple_of(start, LANES), LANES)] = part[here, z, x]
+
+        @pl.when(jnp.logical_not(narrow))
+        def _():
+            for half in range(2):
+                start = wide_at * 2 * LANES + half * LANES
+                out_ref[layer, :, pl.ds(pl.multiple_of(start, LANES), LANES)] = part[here, z, half]
+
+        @pl.when(item + slots < items)
+        def _():
+            @pl.when(has_left)
+            def _():
+                signal(from_right, left)
+
+            @pl.when(has_right)
+            def _():
+                signal(from_left, right)
+
+    for item in range(1, AHEAD):
+        send_wide(jnp.int32(item))
+
+    @pl.loop(0, items + line - 1)
+    def _(step):
+        def guard(item, action):
+            pl.when(jnp.logical_and(item >= 0, item < items))(lambda: action(item))
+
+        guard(step + AHEAD, send_wide)
+        guard(step - (line - 1), finish)
+        for stage in reversed(range(1, line - 1)):
+            guard(step - stage, functools.partial(hop, stage=stage))
+
+        def begin(item):
+            form(item)
+            hop(item, 0)
+
+        guard(step, begin)
+
+    for number in range(2 * layers):
+        b_copy(number).wait()
+        start = wide_per * 2 * LANES + (number % 2) * LANES
+        out_ref[number // 2, :, start : start + LANES] += br[number]
+
+    def square_rows(index, total):
+        layer = index // (rows // 8)
+        at = pl.multiple_of(index % (rows // 8) * 8, 8)
+        for piece in range(cols // LANES):
+            value = out_ref[layer, pl.ds(at, 8), piece * LANES : (piece + 1) * LANES]
+            total = total + value * value
+        return total
+
+    def spread(src, landing, send, recv, axis, index, size):
+        copies = []
+        for offset in range(1, size):
+            copies.append(
+                pltpu.make_async_remote_copy(
+                    src_ref=src, dst_ref=landing.at[offset - 1],
+                    send_sem=send.at[offset - 1], recv_sem=recv.at[offset - 1],
+                    device_id={axis: lax.rem(index + offset, size)},
+                    device_id_type=pl.DeviceIdType.MESH,
+                )
+            )
+        for copy in copies:
+            copy.start()
+        for copy in copies:
+            copy.wait()
+        total = src[...]
+        for offset in range(1, size):
+            total = total + landing[offset - 1]
+        return total
+
+    own_sq[...] = lax.fori_loop(
+        0, layers * rows // 8, square_rows, jnp.zeros((8, LANES), jnp.float32)
+    )
+    sum_sq[...] = spread(own_sq, col_sq, cs_sem, cr_sem, "col", mine, col_count)
+    sq_ref[...] = spread(sum_sq, dp_sq, ds_sem, dr_sem, "dp", me, count)
+
+
+def reduced_gradient(activations, cotangent, mesh_shape):
+    count = mesh_shape["dp"]
+    col_count = mesh_shape["col"]
+    layers, tokens, cols = activations.shape
+    line = count // 2
+    rows = cotangent.shape[2] // count
+    slots = line + 2
+    cot = cotangent.reshape(layers, tokens, line, 2, rows).transpose(0, 3, 2, 4, 1)
+    block = (line, 2, rows, LANES)
+    dma = pltpu.SemaphoreType.DMA
+    vmem = pl.BlockSpec(memory_space=pltpu.VMEM)
+    return pl.pallas_call(
+        functools.partial(reduce_kernel, count, col_count),
+        out_shape=(
+            jax.ShapeDtypeStruct((layers, rows, cols), jnp.float32),
+            jax.ShapeDtypeStruct((8, LANES), jnp.float32),
+        ),
+        in_specs=[vmem, vmem],
+        out_specs=(vmem, vmem),
+        scratch_shapes=[
+            pltpu.VMEM((XSLOTS,) + block, jnp.float32),
+            pltpu.VMEM((XSLOTS,) + block, jnp.float32),
+            pltpu.VMEM((slots,) + block, jnp.float32),
+            pltpu.VMEM((slots, line + 1) + block[1:], jnp.float32),
+            pltpu.VMEM((2 * layers, rows, LANES), jnp.float32),
+            pltpu.VMEM((2 * layers, rows, LANES), jnp.float32),
+            pltpu.VMEM((8, LANES), jnp.float32),
+            pltpu.VMEM((8, LANES), jnp.float32),
+            pltpu.VMEM((col_count - 1, 8, LANES), jnp.float32),
+            pltpu.VMEM((count - 1, 8, LANES), jnp.float32),
+            dma((XSLOTS,)), dma((XSLOTS,)),
+            dma((slots, line)), dma((slots, line)), dma((slots, line)), dma((slots, line)),
+            dma((2 * layers,)), dma((2 * layers,)),
+            dma((col_count - 1,)), dma((col_count - 1,)), dma((count - 1,)), dma((count - 1,)),
+            pltpu.SemaphoreType.REGULAR, pltpu.SemaphoreType.REGULAR, pltpu.SemaphoreType.REGULAR,
+        ],
+        compiler_params=pltpu.CompilerParams(
+            collective_id=0, has_side_effects=True, vmem_limit_bytes=62 * 2**20
+        ),
+    )(cot, activations)
+
 
 def local(
-    activations, cotangent, master_weights, moment_codes, square_codes, moment_scales, square_scales
+    mesh_shape, activations, cotangent, master_weights, moment_codes, square_codes, moment_scales, square_scales
 ):
     layer_count = activations.shape[0]
     shard_rows = master_weights.shape[1]
     shard_cols = master_weights.shape[2]
     block_count = moment_scales.shape[2]
-    pieces = []
-    for layer_index in range(layer_count):
-
-        def layer_term(row_start, row_count, layer_index=layer_index):
-            cot_rows = cotangent[layer_index]
-            return lax.dot_general(
-                cot_rows,
-                activations[layer_index],
-                (((0,), (0,)), ((), ())),
-                preferred_element_type=jnp.float32,
-            )
-
-        pieces.append(
-            lax.psum_scatter(
-                layer_term(jnp.int32(0), lax.axis_size("dp") * shard_rows),
-                "dp",
-                scatter_dimension=0,
-                tiled=True,
-            )
-        )
-    gradient = jnp.stack(pieces)
-    local_sq = jnp.sum(gradient * gradient)
-    total_sq = lax.psum(local_sq, ("dp", "col"))
+    gradient, squares = reduced_gradient(activations, cotangent, mesh_shape)
+    total_sq = jnp.sum(squares)
     rms = jnp.sqrt(total_sq / float(LAYERS * KV * D) + norm_eps)
     clip_factor = jnp.minimum(1.0, 1.0 / rms)
     correct_one = 1.0 - beta_one**STEP
@@ -111,4 +412,4 @@
         P(None, "dp", None),
         P(None, "dp", None),
     )
-    return jax.shard_map(local, mesh=mesh, in_specs=in_specs, out_specs=out_specs, check_vma=False)
+    return jax.shard_map(functools.partial(local, dict(mesh.shape)), mesh=mesh, in_specs=in_specs, out_specs=out_specs, check_vma=False)

time: 668 us -> 430 us (0.64)
  waiting for transfers between devices: 550 us -> 0 us
  Pallas kernels: 0 us -> 376 us
  blocking collectives: 50.1 us -> 10.1 us
  matrix products: 29.9 us -> 0 us
  local copies, waits for them, and re-layouts: 0.01 us -> 19.3 us
  between operations: 14.8 us -> 1.4 us
    reduce_scatter x2 -> x0, waiting for transfers between devices: 550 us -> none  [local(): lax.psum_scatter(layer_term(jnp.int32(0), lax.axis_size('dp') * shard_row...]
    pallas_call x0 -> x1, Pallas kernels: none -> 376 us  [reduced_gradient(): pl.pallas_call(functools.partial(reduce_kernel, count, col_count), out_sh...]
    psum x1 -> x0, blocking collectives: 39.7 us -> none  [local(): total_sq = lax.psum(local_sq, ('dp', 'col'))]
    dot_general x2 -> x0, matrix products: 29.9 us -> none  [layer_term(): lax.dot_general(cot_rows, activations[layer_index], (((0,), (0,)), ((), (...]
    unnamed x6 -> x7, local copies, waits for them, and re-layouts: 0.01 us -> 12.5 us
    another operation x2 -> x1, other arithmetic: 10.8 us -> 2.28 us  [local(): jnp.stack(outs_weights)]
    reshape x0 -> x1, local copies, waits for them, and re-layouts: none -> 6.84 us  [reduced_gradient(): cotangent.reshape(layers, tokens, line, 2, rows).transpose(0, 3, 2, 4, 1)]
  transfers between devices with their start and end apart: 2 -> 0, of which waited for: 2 -> 0; matrix products, arithmetic and copies ran while one was open for 2% -> 0% of each run, Pallas kernels for 0% -> 0%
where the time goes in v1:
time: 430 us; the launch traced here: 429 us
  Pallas kernels  376 us (87%)
  other arithmetic  22.7 us (5%)
  local copies, waits for them, and re-layouts  19.3 us (4%)
  blocking collectives  10.1 us (2%)
    pallas_call x1, Pallas kernels, reduced_gradient(): pl.pallas_call(functools.partial(reduce_kernel, count, col_count), out_sh...  376 us
    unnamed x7, local copies, waits for them, and re-layouts  12.5 us
    pmax x1, blocking collectives, local(): moment_max, square_max = lax.pmax((moment_part, square_part), 'col')  10.1 us

profile of v1, /device:TPU:0, one launch (start us, length us, event | category | flops | bytes accessed | tf_op | source)
XLA Modules:
  0.0 429.3 jit_solution(12910254150144801660)
XLA Ops:
  0.7 0.8 fusion.28
  1.5 11.4 %copy.12 = bf16[2,896,2048]{1,2,0:T(8,128)(2,1)} copy(bf16[2,896,2048]{2,1,0:T(8,128)(2,1)} %param.8) | data formatting | bytes 14680064 | tf_op args[1]
  12.9 6.8 %copy.15 = bf16[2,896,4,2,256]{1,4,2,3,0:T(8,128)(2,1)} copy(bf16[2,896,4,2,256]{1,4,3,2,0:T(8,128)(2,1)} %bitcast.79) | data formatting | bytes 14680064 | tf_op jit(solution)/shard_map/reshape | solution.py:309
  19.7 375.7 %shard_map.110 = (f32[2,256,2048]{2,1,0:T(8,128)}, f32[8,128]{1,0:T(8,128)}) custom-call(bf16[2,2,4,256,896]{4,3,2,1,0:T(8,128)(2,1)} %bitcast.78, bf16[2,896,2048]{2,1,0:T(8,128)(2,1)} %act_ref.1), custom_call_target="tpu_custom_call" | custom-call | tf_op jit(solution)/shard_map/pallas_call | solution.py:313
  395.4 1.3 reduce_sum.82
  397.3 0.0 copy-start.1
  397.4 5.6 %fusion.12 = (f32[256]{0:T(256)S(1)}, f32[256]{0:T(256)S(1)}, f32[256]{0:T(256)S(1)}, f32[256]{0:T(256)S(1)}) fusion(f32[2,256,2048]{2,1,0:T(8,128)} %get-tuple-element.8, f32[256]{0:T(256)S(1)} %get-tuple-element.15, f32[]{:T(128)S(6)} %min.3, bf16[2,256,2048]{2,1,0:T(8,128)(2,1)} %param.11, f32[256]{0:T(256)S(1)} %get-tuple-element.16, ...), kind=kLoop, calls=%fused_computation.26 | loop fusion | flops 15727616 | bytes 8396804 | tf_op jit(solution)/shard_map/reduce_max | solution.py:369
  403.0 0.1 broadcast_multiply_fusion
  403.0 10.1 %all-reduce = (f32[256,4]{0,1:T(4,128)S(1)}, f32[256,4]{0,1:T(4,128)S(1)}, f32[256,4]{0,1:T(4,128)S(1)}, f32[256,4]{0,1:T(4,128)S(1)}) all-reduce(f32[256,4]{0,1:T(4,128)S(1)} %get-tuple-element.37, f32[256,4]{0,1:T(4,128)S(1)} %get-tuple-element.36, f32[256,4]{0,1:T(4,128)S(1)} %get-tuple-element.38, ...), channel_id=1, replica_groups=mesh['dp'=8,'col'=4] {'col'}, use_global_device_ids=true, to_apply=%region_12.13 | all-reduce | flops 4096 | bytes 32768 | tf_op jit(solution)/shard_map/pmax | solution.py:376
  413.2 0.1 multiply_reduce_fusion.1
  413.3 0.6 pad_maximum_fusion.3
  413.9 0.0 copy-done.1
  413.9 0.0 copy-start
  413.9 0.0 copy-start.2
  413.9 2.7 divide_convert_fusion.1
  416.6 0.4 copy-done
  417.0 0.7 copy-done.2
  417.7 6.3 %multiply_subtract_fusion.1 = (f32[1,256,2048]{2,1,0:T(8,128)S(1)}, f32[1,256,2048]{2,1,0:T(8,128)S(1)}, bf16[1,256,2048]{2,1,0:T(8,128)(2,1)S(1)}, bf16[1,256,2048]{2,1,0:T(8,128)(2,1)S(1)}) fusion(f32[2,256,2048]{2,1,0:T(8,128)} %param.9, f32[2,256,2048]{2,1,0:T(8,128)S(1)} %copy-done, f32[]{:T(128)S(6)} %min.3, f32[256]{0:T(256)S(1)} %get-tuple-element.24, ...), kind=kLoop, calls=%fused_computation.50 | loop fusion | flops 23068672 | bytes 18880516 | tf_op jit(solution)/shard_map/sub | solution.py:383
  424.0 2.3 pad_maximum_fusion
  426.3 1.5 pad_maximum_fusion.2
  427.8 1.5 pad_maximum_fusion.1
  (3 shorter events, 0.0 us)
Async XLA Ops:
  397.3 16.6 %copy-start.1 = (bf16[2,256,2048]{2,1,0:T(8,128)(2,1)S(1)}, bf16[2,256,2048]{2,1,0:T(8,128)(2,1)}, u32[]{:S(2)}) copy-start(bf16[2,256,2048]{2,1,0:T(8,128)(2,1)} %param.10) | copy-start | bytes 6291460
  413.9 3.1 copy-start
  413.9 3.8 copy-start.2
